TPU v7x, 32 devices: a whole 2x2x4 slice. The times are simulated.
32 devices in a mesh: seq: 8 (over z, x), rows: 4 (over y, core).
Axes of the slice: x: 2, y: 2, z: 4, core: 2. Of those that a mesh axis runs over, the one named last changes fastest.
Arguments:
- attn_in: bfloat16 [8192, 8192], P(('seq', 'rows')), may hold values from -6 to 6
- attn_out: bfloat16 [8192, 8192], P(('seq', 'rows')), may hold values from -6 to 6
- valid: int32 [8192], P(('seq', 'rows')), may hold values 0 or 1
- w_qkv: bfloat16 [10240, 8192], P('rows', 'seq'), may hold values from -6 to 6
- w_out: bfloat16 [8192, 8192], P('rows', 'seq'), may hold values from -6 to 6
- qkv_ranks: int32 [10240], P('rows'), may hold values from 3072 to 5120
- out_ranks: int32 [8192], P('rows'), may hold values from 3072 to 5120
Outputs:
- qkv_margins: float32 [10240, 8192], P('rows', 'seq')
- out_margins: float32 [8192, 8192], P('rows', 'seq')
Inputs may be any that keep to these rules, and one draw needn't show every extreme that they name: `qkv_ranks`: each row keeps between three and five eighths of its 8192 weights. `out_ranks`: each row keeps between three and five eighths of its 8192 weights.
All inputs are finite; a program needn't handle non-finite values. No bound on the sum of `valid` on one device may be relied on, other than what follows from the above.
Results may differ from a plain program's by a relative error of at most 0.0003.
Values may be sent and summed in bfloat16 or wider, within the bound.
A program may use at most 128 MiB of HBM per device.

v0:
```python
import jax
import jax.numpy as jnp
from jax import lax
from jax.sharding import PartitionSpec as P

EPS = 1e-06


def tile_scores(weights, norm):
    return jnp.abs(weights.astype(jnp.float32)) * norm[None, :]


def row_limits(scores, ranks):
    lower = jnp.zeros((scores.shape[0],), jnp.float32)
    upper = jnp.max(scores, axis=1) + 1.0

    def bisect(step, state):
        low, high = state
        middle = 0.5 * (low + high)
        counted = jnp.sum((scores >= middle[:, None]).astype(jnp.int32), axis=1)
        rising = counted >= ranks
        return (jnp.where(rising, middle, low), jnp.where(rising, high, middle))

    lower, upper = lax.fori_loop(0, 24, bisect, (lower, upper))
    start = jnp.min(jnp.where(scores >= lower[:, None], scores, jnp.inf), axis=1)

    def strictly_above(candidate):
        return jnp.sum((scores > candidate[:, None]).astype(jnp.int32), axis=1)

    def unfinished(candidate):
        return jnp.any(strictly_above(candidate) >= ranks)

    def advance(candidate):
        further = strictly_above(candidate) >= ranks
        following = jnp.min(jnp.where(scores > candidate[:, None], scores, jnp.inf), axis=1)
        return jnp.where(further, following, candidate)

    return lax.while_loop(unfinished, advance, start)


def clipped(scores, limits):
    return jnp.maximum(scores - limits[:, None], 0.0)


def per_device(attn_in, attn_out, valid, w_qkv, w_out, qkv_ranks, out_ranks):
    weight = valid.astype(jnp.float32)[:, None]

    def squares(acts):
        acts32 = acts.astype(jnp.float32)
        return jnp.sum(acts32 * acts32 * weight, axis=0)

    partial_sums = jnp.stack([squares(attn_in), squares(attn_out)])
    total_tokens = attn_in.shape[0] * lax.axis_size("seq") * lax.axis_size("rows")
    seq_index = lax.axis_index("seq")
    totals = lax.psum(partial_sums, ("seq", "rows"))
    full_norm = jnp.sqrt(totals / total_tokens + EPS)
    qkv_whole, out_whole = (
        lax.all_to_all(w_qkv, "seq", split_axis=0, concat_axis=1, tiled=True),
        lax.all_to_all(w_out, "seq", split_axis=0, concat_axis=1, tiled=True),
    )
    qkv_rows = tile_scores(qkv_whole, full_norm[0])
    out_rows = tile_scores(out_whole, full_norm[1])
    qkv_count = qkv_rows.shape[0]
    out_count = out_rows.shape[0]
    qkv_mine = lax.dynamic_slice_in_dim(qkv_ranks, seq_index * qkv_count, qkv_count)
    out_mine = lax.dynamic_slice_in_dim(out_ranks, seq_index * out_count, out_count)
    qkv_limits = row_limits(qkv_rows, qkv_mine)
    out_limits = row_limits(out_rows, out_mine)
    qkv_result, out_result = (
        lax.all_to_all(
            clipped(qkv_rows, qkv_limits), "seq", split_axis=1, concat_axis=0, tiled=True
        ),
        lax.all_to_all(
            clipped(out_rows, out_limits), "seq", split_axis=1, concat_axis=0, tiled=True
        ),
    )
    return (qkv_result, out_result)


def solution(mesh):
    placed = (
        P(("seq", "rows"), None),
        P(("seq", "rows"), None),
        P(("seq", "rows")),
        P("rows", "seq"),
        P("rows", "seq"),
        P("rows"),
        P("rows"),
    )
    return jax.shard_map(
        per_device,
        mesh=mesh,
        in_specs=placed,
        out_specs=(P("rows", "seq"), P("rows", "seq")),
        check_vma=False,
    )
```

profile of v0, /device:TPU:0, one launch (start us, length us, event | category | flops | bytes accessed | tf_op | source)
XLA Modules:
  0.0 824.9 jit_solution(17134786051954232279)
XLA Ops:
  7.2 7.3 all-to-all-start.2
  22.7 165.7 %all-reduce.2.cloned.1.call-done = f32[2,8192]{1,0:T(2,128)} async-done(((f32[2,8192]{1,0:T(2,128)}), f32[2,8192]{1,0:T(2,128)}) %all-reduce.2.cloned.1.call-update) | async-done | bytes 65552 | tf_op jit(solution)/shard_map/psum | solution.py:55
  189.5 5.4 all-to-all-start
  204.4 122.3 %while.43 = (s32[]{:T(128)}, f32[256]{0:T(256)S(1)}, f32[256]{0:T(256)S(1)}, f32[256,8192]{1,0:T(8,128)}, s32[256]{0:T(256)}, /*index=5*/s32[]{:T(128)}, s32[]{:T(128)}) while((s32[]{:T(128)}, f32[256]{0:T(256)S(1)}, f32[256]{0:T(256)S(1)}, f32[256,8192]{1,0:T(8,128)}, s32[256]{0:T(256)}, /*index=5*/s32[]{:T(128)}, ...), condition=%wide.region_17.18_spmd.clone, body=%wide.region_15.17_spmd.clone.sunk | while | flops 6292995 | bytes 8402528 | solution.py:24
  331.2 6.6 while.39
  337.8 7.1 fusion.11
  344.9 21.1 %all-to-all-start.3 = ((f32[256,8,1024]{2,0,1:T(8,128)}), f32[256,8,1024]{2,0,1:T(8,128)}, u32[]{:S(2)}, u32[]{:S(2)}) async-start(f32[256,8,1024]{2,0,1:T(8,128)} %fusion.11), calls=%async_computation.3 | async-start | bytes 16777216 | tf_op jit(solution)/shard_map/all_to_all | solution.py:73
  370.2 5.2 copy.11
  375.4 9.7 %broadcast_multiply_fusion = f32[320,8192]{1,0:T(8,128)} fusion(f32[320,8192]{1,0:T(8,128)} %bitcast.30, f32[8192]{0:T(1024)S(1)} %bitcast.34), kind=kLoop, calls=%fused_computation.39 | loop fusion | flops 2621440 | bytes 21004288 | tf_op jit(solution)/shard_map/mul | solution.py:10
  385.0 141.9 %while.42 = (s32[]{:T(128)}, f32[320]{0:T(512)S(1)}, f32[320]{0:T(512)S(1)}, f32[320,8192]{1,0:T(8,128)}, s32[320]{0:T(512)}, /*index=5*/s32[]{:T(128)}, s32[]{:T(128)}) while((s32[]{:T(128)}, f32[320]{0:T(512)S(1)}, f32[320]{0:T(512)S(1)}, f32[320,8192]{1,0:T(8,128)}, s32[320]{0:T(512)}, /*index=5*/s32[]{:T(128)}, s32[]{:T(128)}) %tuple.71), condition=%wide.region_6.7_spmd.clone, body=%wide.region_4.6_spmd.clone.sunk | while | flops 7866243 | bytes 10503136 | solution.py:24
  391.0 5.2 convert_reduce_fusion.6
  396.9 5.2 convert_reduce_fusion.6
  402.8 5.2 convert_reduce_fusion.6
  426.4 5.2 convert_reduce_fusion.6
  432.4 5.2 convert_reduce_fusion.6
  438.3 5.2 convert_reduce_fusion.6
  444.2 5.2 convert_reduce_fusion.6
  526.9 5.3 fusion.5
  532.2 24.8 %while.37 = (f32[320]{0:T(512)}, f32[320,8192]{1,0:T(8,128)}, s32[320]{0:T(512)}) while((f32[320]{0:T(512)}, f32[320,8192]{1,0:T(8,128)}, s32[320]{0:T(512)}) %tuple.87), condition=%region_11.14_spmd, body=%region_8.11_spmd | while | flops 23593280 | bytes 73417016 | solution.py:38
  539.6 5.3 fusion.1
  557.0 8.4 %fusion.6 = f32[320,8,1024]{2,0,1:T(8,128)} fusion(bf16[8,320,1024]{2,1,0:T(8,128)(2,1)} %all-to-all-done, f32[320]{0:T(512)} %get-tuple-element.95, f32[8,1024]{1,0:T(8,128)S(1)} %mul.81), kind=kLoop, calls=%fused_computation.25 | loop fusion | flops 13107200 | bytes 15762688 | tf_op jit(solution)/shard_map/max | solution.py:42
  570.6 228.8 %all-to-all-done.1 = f32[320,8,1024]{2,0,1:T(8,128)} async-done(((f32[320,8,1024]{2,0,1:T(8,128)}), f32[320,8,1024]{2,0,1:T(8,128)}, u32[]{:S(2)}, u32[]{:S(2)}) %all-to-all-start.1) | async-done | bytes 10485792 | tf_op jit(solution)/shard_map/all_to_all | solution.py:70
  799.4 10.3 %copy.40 = f32[2560,1024]{1,0:T(8,128)} copy(f32[2560,1024]{1,0:T(8,128)} %bitcast.7) | data formatting | bytes 20971520
  809.6 8.4 %copy.41 = f32[2048,1024]{1,0:T(8,128)} copy(f32[2048,1024]{1,0:T(8,128)} %bitcast.13) | data formatting | bytes 16777216
  (221 shorter events, 283.2 us)
Async XLA Ops:
  7.2 7.4 copy-start.2
  7.2 182.3 %all-to-all-start.2 = ((bf16[8,256,1024]{2,1,0:T(8,128)(2,1)}), bf16[8,256,1024]{2,1,0:T(8,128)(2,1)}, u32[]{:S(2)}, u32[]{:S(2)}) async-start(bf16[8,256,1024]{2,1,0:T(8,128)(2,1)} %bitcast.33), calls=%async_computation.2 | async-start | bytes 8388608 | tf_op jit(solution)/shard_map/all_to_all | solution.py:59
  14.5 173.9 %all-reduce.2.cloned.1.call-start = ((), (), s32[]{:S(2)}) async-start(), calls=%async_computation.4 | async-start | bytes 131072 | tf_op jit(solution)/shard_map/psum | solution.py:55
  189.5 155.4 %all-to-all-start = ((bf16[8,320,1024]{2,1,0:T(8,128)(2,1)}), bf16[8,320,1024]{2,1,0:T(8,128)(2,1)}, u32[]{:S(2)}, u32[]{:S(2)}) async-start(bf16[8,320,1024]{2,1,0:T(8,128)(2,1)} %bitcast.32), calls=%async_computation | async-start | bytes 10485760 | tf_op jit(solution)/shard_map/all_to_all | solution.py:58
  344.9 220.5 %all-to-all-start.3 = ((f32[256,8,1024]{2,0,1:T(8,128)}), f32[256,8,1024]{2,0,1:T(8,128)}, u32[]{:S(2)}, u32[]{:S(2)}) async-start(f32[256,8,1024]{2,0,1:T(8,128)} %fusion.11), calls=%async_computation.3 | async-start | bytes 16777216 | tf_op jit(solution)/shard_map/all_to_all | solution.py:73
  539.6 7.0 copy-start
  565.4 233.9 %all-to-all-start.1 = ((f32[320,8,1024]{2,0,1:T(8,128)}), f32[320,8,1024]{2,0,1:T(8,128)}, u32[]{:S(2)}, u32[]{:S(2)}) async-start(f32[320,8,1024]{2,0,1:T(8,128)} %fusion.6), calls=%async_computation.1 | async-start | bytes 20971520 | tf_op jit(solution)/shard_map/all_to_all | solution.py:70
Sparse Core Ops, SparseCore 0:
  21.4 166.8 all-reduce.1
where the time goes:
time: 829 us; the launch traced here: 825 us
  waiting for transfers between devices  394 us (48%)
  other arithmetic  344 us (41%)
  starting transfers between devices  39 us (5%)
  local copies, waits for them, and re-layouts  30.1 us (4%)
  between operations  14.2 us (2%)
    reduce_sum x48, other arithmetic, bisect(): counted = jnp.sum((scores >= middle[:, None]).astype(jnp.int32), axis=1)  229 us
    all_to_all x1, waiting for transfers between devices, per_device(): lax.all_to_all(clipped(qkv_rows, qkv_limits), 'seq', split_axis=1, concat...  229 us
    psum x1, waiting for transfers between devices, per_device(): totals = lax.psum(partial_sums, ('seq', 'rows'))  166 us
    select_n x96, other arithmetic, bisect(): return (jnp.where(rising, middle, low), jnp.where(rising, high, middle))  33.9 us
    all_to_all x1, starting transfers between devices, per_device(): lax.all_to_all(clipped(out_rows, out_limits), 'seq', split_axis=1, concat...  21.1 us
    unnamed x4, local copies, waits for them, and re-layouts  18.7 us
    reduce_sum x4, other arithmetic, strictly_above(): return jnp.sum((scores > candidate[:, None]).astype(jnp.int32), axis=1)  16.6 us
  transfers between devices with their start and end apart: 5, of which 2 were waited for; matrix products, arithmetic and copies ran while one was open for 43% of the time, Pallas kernels for 0%

commit v1 on v0

--- a/solution.py
+++ b/solution.py
@@ -4,6 +4,12 @@
 from jax.sharding import PartitionSpec as P
 
 EPS = 1e-06
+
+
+def swap_blocks(x, name, split, join):
+    pieces = jnp.split(x, lax.axis_size(name), axis=split)
+    got = lax.all_to_all(jnp.stack(pieces), name, 0, 0)
+    return jnp.concatenate(got, axis=join)
 
 
 def tile_scores(weights, norm):
@@ -67,9 +73,7 @@
     qkv_limits = row_limits(qkv_rows, qkv_mine)
     out_limits = row_limits(out_rows, out_mine)
     qkv_result, out_result = (
-        lax.all_to_all(
-            clipped(qkv_rows, qkv_limits), "seq", split_axis=1, concat_axis=0, tiled=True
-        ),
+        swap_blocks(clipped(qkv_rows, qkv_limits), "seq", 1, 0),
         lax.all_to_all(
             clipped(out_rows, out_limits), "seq", split_axis=1, concat_axis=0, tiled=True
         ),

time: 829 us -> 847 us (1.022)
  local copies, waits for them, and re-layouts: 30.1 us -> 51.6 us
    unnamed x4 -> x15, local copies, waits for them, and re-layouts: 18.7 us -> 37.8 us
  transfers between devices with their start and end apart: 5 -> 5, of which waited for: 2 -> 2; matrix products, arithmetic and copies ran while one was open for 43% -> 44% of each run, Pallas kernels for 0% -> 0%
where the time goes in v1:
time: 847 us; the launch traced here: 843 us
  waiting for transfers between devices  395 us (47%)
  other arithmetic  341 us (40%)
  local copies, waits for them, and re-layouts  51.6 us (6%)
  starting transfers between devices  38.9 us (5%)
  between operations  14.2 us (2%)
    reduce_sum x48, other arithmetic, bisect(): counted = jnp.sum((scores >= middle[:, None]).astype(jnp.int32), axis=1)  229 us
    all_to_all x1, waiting for transfers between devices, swap_blocks(): got = lax.all_to_all(jnp.stack(pieces), name, 0, 0)  229 us
    psum x1, waiting for transfers between devices, per_device(): totals = lax.psum(partial_sums, ('seq', 'rows'))  166 us
    unnamed x15, local copies, waits for them, and re-layouts  37.8 us
    select_n x96, other arithmetic, bisect(): return (jnp.where(rising, middle, low), jnp.where(rising, high, middle))  32.6 us
    all_to_all x1, starting transfers between devices, per_device(): lax.all_to_all(clipped(out_rows, out_limits), 'seq', split_axis=1, concat...  21 us
    reduce_sum x4, other arithmetic, strictly_above(): return jnp.sum((scores > candidate[:, None]).astype(jnp.int32), axis=1)  20.2 us
  transfers between devices with their start and end apart: 5, of which 2 were waited for; matrix products, arithmetic and copies ran while one was open for 44% of the time, Pallas kernels for 0%

profile of v1, /device:TPU:0, one launch (start us, length us, event | category | flops | bytes accessed | tf_op | source)
XLA Modules:
  0.0 843.4 jit_solution(9285544346414421268)
XLA Ops:
  7.2 7.3 all-to-all-start.2
  22.6 165.7 %all-reduce.2.cloned.1.call-done = f32[2,8192]{1,0:T(2,128)} async-done(((f32[2,8192]{1,0:T(2,128)}), f32[2,8192]{1,0:T(2,128)}) %all-reduce.2.cloned.1.call-update) | async-done | bytes 65552 | tf_op jit(solution)/shard_map/psum | solution.py:61
  189.6 5.4 all-to-all-start
  204.4 122.3 %while.43 = (s32[]{:T(128)}, f32[256]{0:T(256)S(1)}, f32[256]{0:T(256)S(1)}, f32[256,8192]{1,0:T(8,128)}, s32[256]{0:T(256)}, /*index=5*/s32[]{:T(128)}, s32[]{:T(128)}) while((s32[]{:T(128)}, f32[256]{0:T(256)S(1)}, f32[256]{0:T(256)S(1)}, f32[256,8192]{1,0:T(8,128)}, s32[256]{0:T(256)}, /*index=5*/s32[]{:T(128)}, ...), condition=%wide.region_17.18_spmd.clone, body=%wide.region_15.17_spmd.clone.sunk | while | flops 6292995 | bytes 8402520 | solution.py:30
  331.2 6.5 while.39
  337.7 7.1 fusion.10
  344.9 21.0 %all-to-all-start.3 = ((f32[256,8,1024]{2,0,1:T(8,128)}), f32[256,8,1024]{2,0,1:T(8,128)}, u32[]{:S(2)}, u32[]{:S(2)}) async-start(f32[256,8,1024]{2,0,1:T(8,128)} %fusion.10), calls=%async_computation.3 | async-start | bytes 16777216 | tf_op jit(solution)/shard_map/all_to_all | solution.py:77
  365.9 8.0 fusion.8
  379.0 5.7 broadcast_multiply_fusion
  386.0 140.6 %while.42 = (s32[]{:T(128)}, f32[320]{0:T(512)S(1)}, f32[320]{0:T(512)S(1)}, f32[320,8192]{1,0:T(8,128)}, s32[320]{0:T(512)}, /*index=5*/s32[]{:T(128)}, s32[]{:T(128)}) while((s32[]{:T(128)}, f32[320]{0:T(512)S(1)}, f32[320]{0:T(512)S(1)}, f32[320,8192]{1,0:T(8,128)}, s32[320]{0:T(512)}, /*index=5*/s32[]{:T(128)}, s32[]{:T(128)}) %tuple.71), condition=%wide.region_6.7_spmd.clone, body=%wide.region_4.6_spmd.clone.sunk | while | flops 7866243 | bytes 10503128 | solution.py:30
  391.9 5.2 convert_reduce_fusion.6
  403.6 5.2 convert_reduce_fusion.6
  409.5 5.2 convert_reduce_fusion.6
  421.2 5.2 convert_reduce_fusion.6
  432.9 5.2 convert_reduce_fusion.6
  438.8 5.2 convert_reduce_fusion.6
  526.6 5.3 fusion.5
  531.9 25.1 %while.37 = (f32[320]{0:T(512)}, f32[320,8192]{1,0:T(8,128)}, s32[320]{0:T(512)}) while((f32[320]{0:T(512)}, f32[320,8192]{1,0:T(8,128)}, s32[320]{0:T(512)}) %tuple.87), condition=%region_11.14_spmd, body=%region_8.11_spmd | while | flops 23593280 | bytes 73417016 | solution.py:44
  531.9 5.3 convert_reduce_fusion
  539.9 5.3 fusion
  557.0 6.6 subtract_maximum_fusion
  589.0 228.8 %all-to-all-done.1 = f32[8,320,1024]{2,1,0:T(8,128)} async-done(((f32[8,320,1024]{2,1,0:T(8,128)}), f32[8,320,1024]{2,1,0:T(8,128)}, u32[]{:S(2)}, u32[]{:S(2)}) %all-to-all-start.1) | async-done | bytes 10485792 | tf_op jit(solution)/shard_map/all_to_all | solution.py:11
  817.8 10.3 %copy.50 = f32[2560,1024]{1,0:T(8,128)} copy(f32[2560,1024]{1,0:T(8,128)} %bitcast.14) | data formatting | bytes 20971520
  828.1 8.4 %copy.51 = f32[2048,1024]{1,0:T(8,128)} copy(f32[2048,1024]{1,0:T(8,128)} %bitcast.20) | data formatting | bytes 16777216
  (233 shorter events, 304.8 us)
Async XLA Ops:
  7.2 7.4 copy-start.4
  7.2 182.4 %all-to-all-start.2 = ((bf16[8,256,1024]{2,1,0:T(8,128)(2,1)}), bf16[8,256,1024]{2,1,0:T(8,128)(2,1)}, u32[]{:S(2)}, u32[]{:S(2)}) async-start(bf16[8,256,1024]{2,1,0:T(8,128)(2,1)} %bitcast.61), calls=%async_computation.2 | async-start | bytes 8388608 | tf_op jit(solution)/shard_map/all_to_all | solution.py:65
  14.5 173.9 %all-reduce.2.cloned.1.call-start = ((), (), s32[]{:S(2)}) async-start(), calls=%async_computation.4 | async-start | bytes 131072 | tf_op jit(solution)/shard_map/psum | solution.py:61
  189.6 155.3 %all-to-all-start = ((bf16[8,320,1024]{2,1,0:T(8,128)(2,1)}), bf16[8,320,1024]{2,1,0:T(8,128)(2,1)}, u32[]{:S(2)}, u32[]{:S(2)}) async-start(bf16[8,320,1024]{2,1,0:T(8,128)(2,1)} %bitcast.60), calls=%async_computation | async-start | bytes 10485760 | tf_op jit(solution)/shard_map/all_to_all | solution.py:64
  344.9 239.0 %all-to-all-start.3 = ((f32[256,8,1024]{2,0,1:T(8,128)}), f32[256,8,1024]{2,0,1:T(8,128)}, u32[]{:S(2)}, u32[]{:S(2)}) async-start(f32[256,8,1024]{2,0,1:T(8,128)} %fusion.10), calls=%async_computation.3 | async-start | bytes 16777216 | tf_op jit(solution)/shard_map/all_to_all | solution.py:77
  379.0 7.0 copy-start.2
  531.9 25.1 %copy-start.3 = (f32[8,40,8,1024]{3,2,0,1:T(8,128)S(1)}, f32[8,40,8,1024]{3,2,0,1:T(8,128)}, u32[]{:S(2)}) copy-start(f32[8,40,8,1024]{3,2,0,1:T(8,128)} %copy-done.2) | copy-start | bytes 31457284
  539.9 7.0 copy-start
  583.9 234.0 %all-to-all-start.1 = ((f32[8,320,1024]{2,1,0:T(8,128)}), f32[8,320,1024]{2,1,0:T(8,128)}, u32[]{:S(2)}, u32[]{:S(2)}) async-start(f32[8,320,1024]{2,1,0:T(8,128)} %fusion.14), calls=%async_computation.1 | async-start | bytes 20971520 | tf_op jit(solution)/shard_map/all_to_all | solution.py:11
Sparse Core Ops, SparseCore 0:
  21.4 166.9 all-reduce.1

commit v2 on v0

--- a/solution.py
+++ b/solution.py
@@ -52,7 +52,8 @@
     partial_sums = jnp.stack([squares(attn_in), squares(attn_out)])
     total_tokens = attn_in.shape[0] * lax.axis_size("seq") * lax.axis_size("rows")
     seq_index = lax.axis_index("seq")
-    totals = lax.psum(partial_sums, ("seq", "rows"))
+    parts = lax.all_gather(partial_sums, ("seq", "rows"), axis=0, tiled=False)
+    totals = parts.sum(axis=0)
     full_norm = jnp.sqrt(totals / total_tokens + EPS)
     qkv_whole, out_whole = (
         lax.all_to_all(w_qkv, "seq", split_axis=0, concat_axis=1, tiled=True),

time: 829 us -> 770 us (0.929)
  waiting for transfers between devices: 394 us -> 335 us
    psum x1 -> x0, waiting for transfers between devices: 166 us -> none  [per_device(): totals = lax.psum(partial_sums, ('seq', 'rows'))]
    all_gather x0 -> x1, waiting for transfers between devices: none -> 109 us  [per_device(): parts = lax.all_gather(partial_sums, ('seq', 'rows'), axis=0, tiled=False)]
  transfers between devices with their start and end apart: 5 -> 5, of which waited for: 2 -> 2; matrix products, arithmetic and copies ran while one was open for 43% -> 46% of each run, Pallas kernels for 0% -> 0%
where the time goes in v2:
time: 770 us; the launch traced here: 766 us
  other arithmetic  345 us (45%)
  waiting for transfers between devices  335 us (44%)
  starting transfers between devices  38.2 us (5%)
  local copies, waits for them, and re-layouts  30.1 us (4%)
  between operations  14.2 us (2%)
    reduce_sum x48, other arithmetic, bisect(): counted = jnp.sum((scores >= middle[:, None]).astype(jnp.int32), axis=1)  229 us
    all_to_all x1, waiting for transfers between devices, per_device(): lax.all_to_all(clipped(qkv_rows, qkv_limits), 'seq', split_axis=1, concat...  226 us
    all_gather x1, waiting for transfers between devices, per_device(): parts = lax.all_gather(partial_sums, ('seq', 'rows'), axis=0, tiled=False)  109 us
    select_n x96, other arithmetic, bisect(): return (jnp.where(rising, middle, low), jnp.where(rising, high, middle))  33.9 us
    all_to_all x1, starting transfers between devices, per_device(): lax.all_to_all(clipped(out_rows, out_limits), 'seq', split_axis=1, concat...  21.1 us
    unnamed x4, local copies, waits for them, and re-layouts  18.7 us
    reduce_sum x4, other arithmetic, strictly_above(): return jnp.sum((scores > candidate[:, None]).astype(jnp.int32), axis=1)  16.6 us
    max x2, other arithmetic, clipped(): return jnp.maximum(scores - limits[:, None], 0.0)  15.6 us
  transfers between devices with their start and end apart: 5, of which 2 were waited for; matrix products, arithmetic and copies ran while one was open for 46% of the time, Pallas kernels for 0%

profile of v2, /device:TPU:0, one launch (start us, length us, event | category | flops | bytes accessed | tf_op | source)
XLA Modules:
  0.0 766.0 jit_solution(8481517645163915200)
XLA Ops:
  7.2 7.3 all-to-all-start.2
  22.7 109.1 %all-gather.4.cloned.1.call-done = f32[32,2,8192]{2,1,0:T(2,128)} async-done(((f32[1,2,8192]{2,1,0:T(2,128)}), f32[32,2,8192]{2,1,0:T(2,128)}) %all-gather.4.cloned.1.call-update) | async-done | bytes 2097168 | tf_op jit(solution)/shard_map/all_gather | solution.py:55
  148.6 122.3 %while.43 = (s32[]{:T(128)}, f32[256]{0:T(256)S(1)}, f32[256]{0:T(256)S(1)}, f32[256,8192]{1,0:T(8,128)}, s32[256]{0:T(256)}, /*index=5*/s32[]{:T(128)}, s32[]{:T(128)}) while((s32[]{:T(128)}, f32[256]{0:T(256)S(1)}, f32[256]{0:T(256)S(1)}, f32[256,8192]{1,0:T(8,128)}, s32[256]{0:T(256)}, /*index=5*/s32[]{:T(128)}, ...), condition=%wide.region_17.18_spmd.clone, body=%wide.region_15.17_spmd.clone.sunk | while | flops 6292995 | bytes 8402528 | solution.py:24
  275.4 6.6 while.39
  282.0 7.1 fusion.11
  289.1 21.1 %all-to-all-start.3 = ((f32[256,8,1024]{2,0,1:T(8,128)}), f32[256,8,1024]{2,0,1:T(8,128)}, u32[]{:S(2)}, u32[]{:S(2)}) async-start(f32[256,8,1024]{2,0,1:T(8,128)} %fusion.11), calls=%async_computation.3 | async-start | bytes 16777216 | tf_op jit(solution)/shard_map/all_to_all | solution.py:74
  314.3 5.2 copy.13
  319.5 9.7 %broadcast_multiply_fusion = f32[320,8192]{1,0:T(8,128)} fusion(f32[320,8192]{1,0:T(8,128)} %bitcast.32, f32[8192]{0:T(1024)S(1)} %bitcast.36), kind=kLoop, calls=%fused_computation.39 | loop fusion | flops 2621440 | bytes 21004288 | tf_op jit(solution)/shard_map/mul | solution.py:10
  329.2 141.9 %while.42 = (s32[]{:T(128)}, f32[320]{0:T(512)S(1)}, f32[320]{0:T(512)S(1)}, f32[320,8192]{1,0:T(8,128)}, s32[320]{0:T(512)}, /*index=5*/s32[]{:T(128)}, s32[]{:T(128)}) while((s32[]{:T(128)}, f32[320]{0:T(512)S(1)}, f32[320]{0:T(512)S(1)}, f32[320,8192]{1,0:T(8,128)}, s32[320]{0:T(512)}, /*index=5*/s32[]{:T(128)}, s32[]{:T(128)}) %tuple.71), condition=%wide.region_6.7_spmd.clone, body=%wide.region_4.6_spmd.clone.sunk | while | flops 7866243 | bytes 10503136 | solution.py:24
  346.9 5.2 convert_reduce_fusion.6
  352.8 5.2 convert_reduce_fusion.6
  358.7 5.2 convert_reduce_fusion.6
  364.6 5.2 convert_reduce_fusion.6
  370.6 5.2 convert_reduce_fusion.6
  376.5 5.2 convert_reduce_fusion.6
  382.4 5.2 convert_reduce_fusion.6
  406.0 5.2 convert_reduce_fusion.6
  471.1 5.3 fusion.5
  476.3 24.8 %while.37 = (f32[320]{0:T(512)}, f32[320,8192]{1,0:T(8,128)}, s32[320]{0:T(512)}) while((f32[320]{0:T(512)}, f32[320,8192]{1,0:T(8,128)}, s32[320]{0:T(512)}) %tuple.87), condition=%region_11.14_spmd, body=%region_8.11_spmd | while | flops 23593280 | bytes 73417016 | solution.py:38
  483.5 5.3 fusion.1
  501.1 8.4 %fusion.6 = f32[320,8,1024]{2,0,1:T(8,128)} fusion(bf16[8,320,1024]{2,1,0:T(8,128)(2,1)} %all-to-all-done, f32[320]{0:T(512)} %get-tuple-element.95, f32[8,1024]{1,0:T(8,128)S(1)} %mul.81), kind=kLoop, calls=%fused_computation.25 | loop fusion | flops 13107200 | bytes 15762688 | tf_op jit(solution)/shard_map/max | solution.py:42
  514.7 225.8 %all-to-all-done.1 = f32[320,8,1024]{2,0,1:T(8,128)} async-done(((f32[320,8,1024]{2,0,1:T(8,128)}), f32[320,8,1024]{2,0,1:T(8,128)}, u32[]{:S(2)}, u32[]{:S(2)}) %all-to-all-start.1) | async-done | bytes 10485792 | tf_op jit(solution)/shard_map/all_to_all | solution.py:71
  740.5 10.3 %copy.41 = f32[2560,1024]{1,0:T(8,128)} copy(f32[2560,1024]{1,0:T(8,128)} %bitcast.8) | data formatting | bytes 20971520
  750.8 8.4 %copy.42 = f32[2048,1024]{1,0:T(8,128)} copy(f32[2048,1024]{1,0:T(8,128)} %bitcast.14) | data formatting | bytes 16777216
  (222 shorter events, 284.2 us)
Async XLA Ops:
  7.2 7.4 copy-start.2
  7.2 127.3 %all-to-all-start.2 = ((bf16[8,256,1024]{2,1,0:T(8,128)(2,1)}), bf16[8,256,1024]{2,1,0:T(8,128)(2,1)}, u32[]{:S(2)}, u32[]{:S(2)}) async-start(bf16[8,256,1024]{2,1,0:T(8,128)(2,1)} %bitcast.35), calls=%async_computation.2 | async-start | bytes 8388608 | tf_op jit(solution)/shard_map/all_to_all | solution.py:60
  14.5 117.4 %all-gather.4.cloned.1.call-start = ((), (), s32[]{:S(2)}) async-start(), calls=%async_computation.4 | async-start | bytes 2162688 | tf_op jit(solution)/shard_map/all_gather | solution.py:55
  134.5 154.7 %all-to-all-start = ((bf16[8,320,1024]{2,1,0:T(8,128)(2,1)}), bf16[8,320,1024]{2,1,0:T(8,128)(2,1)}, u32[]{:S(2)}, u32[]{:S(2)}) async-start(bf16[8,320,1024]{2,1,0:T(8,128)(2,1)} %bitcast.34), calls=%async_computation | async-start | bytes 10485760 | tf_op jit(solution)/shard_map/all_to_all | solution.py:59
  289.1 220.4 %all-to-all-start.3 = ((f32[256,8,1024]{2,0,1:T(8,128)}), f32[256,8,1024]{2,0,1:T(8,128)}, u32[]{:S(2)}, u32[]{:S(2)}) async-start(f32[256,8,1024]{2,0,1:T(8,128)} %fusion.11), calls=%async_computation.3 | async-start | bytes 16777216 | tf_op jit(solution)/shard_map/all_to_all | solution.py:74
  483.5 7.0 copy-start
  509.5 231.0 %all-to-all-start.1 = ((f32[320,8,1024]{2,0,1:T(8,128)}), f32[320,8,1024]{2,0,1:T(8,128)}, u32[]{:S(2)}, u32[]{:S(2)}) async-start(f32[320,8,1024]{2,0,1:T(8,128)} %fusion.6), calls=%async_computation.1 | async-start | bytes 20971520 | tf_op jit(solution)/shard_map/all_to_all | solution.py:71
Sparse Core Ops, SparseCore 0:
  20.1 111.7 all-gather.3
